TPU v7x, 32 devices: a whole 2x2x4 slice. The times are simulated.
32 devices in a mesh: dp: 4 (over x, core), mp: 8 (over z, y).
Axes of the slice: x: 2, y: 2, z: 4, core: 2. Of those that a mesh axis runs over, the one named last changes fastest.
Arguments:
- tokens: bfloat16 [1024, 8192], P('dp'), may hold values from -6 to 6
- norm_gain: float32 [8192], replicated, may hold values from 0.5 to 1.5
- gate_weight: bfloat16 [8192, 28672], P('dp', 'mp'), may hold values from -0.0625 to 0.0625
- gate_mask: int32 [8192, 896], P('dp', 'mp'), may hold values from -2147483648 to 2147483646
- up_weight: bfloat16 [8192, 28672], P('dp', 'mp'), may hold values from -0.0625 to 0.0625
- up_mask: int32 [8192, 896], P('dp', 'mp'), may hold values from -2147483648 to 2147483646
- down_weight: bfloat16 [28672, 8192], P('mp', 'dp'), may hold values from -0.03125 to 0.03125
- down_mask: int32 [28672, 256], P('mp', 'dp'), may hold values from -2147483648 to 2147483647, as said below
Outputs:
- mixed: bfloat16 [1024, 8192], P('mp', 'dp')
- input_norms: float32 [8192], P('dp')
- hidden_norms: float32 [28672], P('mp')
Inputs may be any that keep to these rules, and one draw needn't show every extreme that they name: `down_mask`: in every word each of the eight aligned groups of four bits holds exactly two ones, so exactly two of every four consecutive columns of the down projection are kept.
All inputs are finite; a program needn't handle non-finite values.
Results may differ from a plain program's by a relative error of at most 0.025.
Values may be sent and summed in bfloat16 or wider, within the bound.
A program may use at most 192 MiB of HBM per device.

v0:
```python
import jax
import jax.numpy as jnp
from jax import lax
from jax.sharding import PartitionSpec as P


def keep_entries(weight, packed):
    shifts = jnp.arange(32, dtype=jnp.int32)
    kept_bits = jnp.right_shift(packed[..., None], shifts) & 1
    kept_bits = kept_bits.reshape(weight.shape)
    return jnp.where(kept_bits == 1, weight, jnp.zeros_like(weight))


def on_device(
    tokens, norm_gain, gate_weight, gate_mask, up_weight, up_mask, down_weight, down_mask
):
    values = tokens.astype(jnp.float32)
    scale = lax.rsqrt(jnp.mean(values * values, axis=1, keepdims=True) + 1e-05)
    normed = (values * scale * norm_gain).astype(jnp.bfloat16)
    columns = lax.all_to_all(normed, "dp", split_axis=1, concat_axis=0, tiled=True)
    widened = columns.astype(jnp.float32)
    input_norms = jnp.sqrt(jnp.sum(widened * widened, axis=0))
    gate_kept = keep_entries(gate_weight, gate_mask)
    up_kept = keep_entries(up_weight, up_mask)
    down_kept = keep_entries(down_weight, down_mask)
    units = gate_kept.shape[1]
    gate_part = jnp.dot(columns, gate_kept, preferred_element_type=jnp.float32)
    up_part = jnp.dot(columns, up_kept, preferred_element_type=jnp.float32)
    both_sums = lax.psum_scatter(
        jnp.concatenate([gate_part, up_part], axis=1).astype(jnp.bfloat16),
        "dp",
        scatter_dimension=0,
        tiled=True,
    ).astype(jnp.float32)
    hidden = (jax.nn.silu(both_sums[:, :units]) * both_sums[:, units:]).astype(jnp.bfloat16)
    wide_hidden = hidden.astype(jnp.float32)
    squares = lax.psum(jnp.sum(wide_hidden * wide_hidden, axis=0), "dp")
    hidden_norms = jnp.sqrt(squares)
    partial_out = jnp.dot(
        lax.all_gather(hidden, "dp", axis=0, tiled=True),
        down_kept,
        preferred_element_type=jnp.float32,
    )
    mixed = lax.psum_scatter(
        partial_out.astype(jnp.bfloat16), "mp", scatter_dimension=0, tiled=True
    )
    return (mixed, input_norms, hidden_norms)


def solution(mesh):
    return jax.shard_map(
        on_device,
        mesh=mesh,
        in_specs=(
            P("dp", None),
            P(),
            P("dp", "mp"),
            P("dp", "mp"),
            P("dp", "mp"),
            P("dp", "mp"),
            P("mp", "dp"),
            P("mp", "dp"),
        ),
        out_specs=(P("mp", "dp"), P("dp"), P("mp")),
        check_vma=False,
    )
```

profile of v0, /device:TPU:0, one launch (start us, length us, event | category | flops | bytes accessed | tf_op | source)
XLA Modules:
  0.0 449.8 jit_solution(9891590436069383037)
XLA Ops:
  7.2 6.4 %copy.17 = bf16[256,8192]{0,1:T(8,128)(2,1)} copy(bf16[256,8192]{1,0:T(8,128)(2,1)} %param.8) | data formatting | bytes 8388608 | tf_op args[0]
  13.6 3.3 fusion.9
  16.9 4.2 fusion.11
  21.0 4.9 %all-to-all-start = ((bf16[256,4,2048]{0,2,1:T(8,128)(2,1)}), bf16[256,4,2048]{0,2,1:T(8,128)(2,1)}, u32[]{:S(2)}, u32[]{:S(2)}) async-start(bf16[256,4,2048]{0,2,1:T(8,128)(2,1)} %bitcast.34), calls=%async_computation | async-start | bytes 8388608 | tf_op jit(solution)/shard_map/all_to_all | solution.py:20
  26.0 0.1 shift_right_arithmetic.63
  26.1 20.3 %copy.19 = bf16[2048,3584]{0,1:T(8,128)(2,1)} copy(bf16[2048,3584]{1,0:T(8,128)(2,1)} %param.10) | data formatting | bytes 29360128 | tf_op args[2]
  46.4 20.5 %copy.20 = bf16[2048,3584]{0,1:T(8,128)(2,1)} copy(bf16[2048,3584]{1,0:T(8,128)(2,1)} %param.12) | data formatting | bytes 29360128 | tf_op args[4]
  66.9 28.4 %fusion.6 = (bf16[2048,3584]{0,1:T(8,128)(2,1)}, bf16[2048,3584]{0,1:T(8,128)(2,1)}) fusion(bf16[2048,3584]{0,1:T(8,128)(2,1)} %copy.19, s32[3584]{0:T(1024)S(1)} %shift_right_arithmetic.63, s32[2048,112]{0,1:T(8,128)S(1)} %copy-done.1, bf16[2048,3584]{0,1:T(8,128)(2,1)} %copy.20, s32[2048,112]{0,1:T(8,128)S(1)} %copy-done.2), kind=kLoop, calls=%fused_computation.9 | loop fusion | flops 58720256 | bytes 60569600 | tf_op jit(solution)/shard_map/jit(_where)/select_n | solution.py:11
  95.3 6.3 %copy.18 = bf16[4,256,2048]{2,1,0:T(8,128)(2,1)} copy(bf16[4,256,2048]{1,2,0:T(8,128)(2,1)} %bitcast.1) | data formatting | bytes 8388608 | tf_op jit(solution)/shard_map/all_to_all | solution.py:20
  101.6 23.7 %convolution_convert_fusion.1 = bf16[1024,3584]{1,0:T(8,128)(2,1)} fusion(bf16[1024,2048]{1,0:T(8,128)(2,1)} %bitcast.35, bf16[2048,3584]{0,1:T(8,128)(2,1)} %get-tuple-element.5), kind=kOutput, calls=%fused_computation.20 | convolution fusion | flops 15036055552 | bytes 26214400 | tf_op jit(solution)/shard_map/dot_general | solution.py:27
  125.3 20.5 %convolution_convert_fusion = bf16[1024,3584]{1,0:T(8,128)(2,1)} fusion(bf16[1024,2048]{1,0:T(8,128)(2,1)S(1)} %bitcast.36, bf16[2048,3584]{0,1:T(8,128)(2,1)} %get-tuple-element.6), kind=kOutput, calls=%fused_computation.19 | convolution fusion | flops 15036055552 | bytes 26214400 | tf_op jit(solution)/shard_map/dot_general | solution.py:28
  145.8 12.6 %pad_maximum_fusion = bf16[1024,7168]{1,0:T(8,128)(2,1)} fusion(bf16[1024,3584]{1,0:T(8,128)(2,1)} %convolution_convert_fusion, bf16[1024,3584]{1,0:T(8,128)(2,1)} %convolution_convert_fusion.1), kind=kLoop, calls=%fused_computation.12 | loop fusion | flops 29360128 | bytes 29360128 | tf_op jit(solution)/shard_map/concatenate | solution.py:30
  158.5 117.2 %reduce-scatter.3.cloned.1.call-done = bf16[256,7168]{1,0:T(8,128)(2,1)} async-done(((bf16[1024,7168]{1,0:T(8,128)(2,1)}), bf16[256,7168]{1,0:T(8,128)(2,1)}) %reduce-scatter.3.cloned.1.call-update) | async-done | bytes 3670032 | tf_op jit(solution)/shard_map/reduce_scatter | solution.py:29
  275.7 2.9 convert_element_type.25
  278.6 2.5 multiply_reduce_fusion.1
  281.3 19.5 %copy.21 = bf16[3584,2048]{0,1:T(8,128)(2,1)} copy(bf16[3584,2048]{1,0:T(8,128)(2,1)} %param.14) | data formatting | bytes 29360128 | tf_op args[6]
  300.8 15.1 %fusion.8 = bf16[3584,2048]{0,1:T(8,128)(2,1)} fusion(bf16[3584,2048]{0,1:T(8,128)(2,1)} %copy.21, s32[2048]{0:T(1024)S(1)} %shift_right_arithmetic.72, s32[3584,64]{0,1:T(8,128)S(1)} %copy-done.3), kind=kLoop, calls=%fused_computation.11 | loop fusion | flops 29360128 | bytes 30285824 | tf_op jit(solution)/shard_map/jit(_where)/select_n | solution.py:11
  315.9 17.7 %all-gather.2.cloned.1.call-done = bf16[1024,3584]{1,0:T(8,128)(2,1)} async-done(((bf16[256,3584]{1,0:T(8,128)(2,1)}), bf16[1024,3584]{1,0:T(8,128)(2,1)}) %all-gather.2.cloned.1.call-update) | async-done | bytes 7340048 | tf_op jit(solution)/shard_map/all_gather | solution.py:40
  333.6 21.2 %convolution_convert_fusion.2 = bf16[1024,2048]{1,0:T(8,128)(2,1)} fusion(bf16[1024,3584]{1,0:T(8,128)(2,1)} %all-gather.2.cloned.1.call-done, bf16[3584,2048]{0,1:T(8,128)(2,1)} %fusion.8), kind=kOutput, calls=%fused_computation.21 | convolution fusion | flops 15034482688 | bytes 26214400 | tf_op jit(solution)/shard_map/dot_general | solution.py:39
  354.9 3.1 multiply_reduce_fusion
  357.9 0.6 sqrt.6
  358.6 10.6 %psum.7 = f32[3584]{0:T(1024)S(1)} all-reduce(f32[3584]{0:T(1024)S(1)} %get-tuple-element.3), channel_id=1, replica_groups=mesh['dp'=4,'mp'=8] {'dp'}, use_global_device_ids=true, to_apply=%region_5.6 | all-reduce | flops 3584 | bytes 28672 | tf_op jit(solution)/shard_map/psum | solution.py:37
  369.2 0.6 sqrt.7
  369.8 73.5 %reduce-scatter.5.cloned.1.call-done = bf16[128,2048]{1,0:T(8,128)(2,1)} async-done(((bf16[1024,2048]{1,0:T(8,128)(2,1)}), bf16[128,2048]{1,0:T(8,128)(2,1)}) %reduce-scatter.5.cloned.1.call-update) | async-done | bytes 524304 | tf_op jit(solution)/shard_map/reduce_scatter | solution.py:44
  (21 shorter events, 0.3 us)
Async XLA Ops:
  7.2 9.7 %copy-start.4 = (f32[8192]{0:T(1024)S(1)}, f32[8192]{0:T(1024)}, u32[]{:S(2)}) copy-start(f32[8192]{0:T(1024)} %param.9) | copy-start | bytes 98308
  21.0 74.2 %all-to-all-start = ((bf16[256,4,2048]{0,2,1:T(8,128)(2,1)}), bf16[256,4,2048]{0,2,1:T(8,128)(2,1)}, u32[]{:S(2)}, u32[]{:S(2)}) async-start(bf16[256,4,2048]{0,2,1:T(8,128)(2,1)} %bitcast.34), calls=%async_computation | async-start | bytes 8388608 | tf_op jit(solution)/shard_map/all_to_all | solution.py:20
  25.9 249.8 %reduce-scatter.3.cloned.1.call-start = ((), (), s32[]{:S(2)}) async-start(), calls=%async_computation.3 | async-start | bytes 18350080 | tf_op jit(solution)/shard_map/reduce_scatter | solution.py:29
  46.4 20.5 %copy-start.1 = (s32[2048,112]{0,1:T(8,128)S(1)}, s32[2048,112]{0,1:T(8,128)}, u32[]{:S(2)}) copy-start(s32[2048,112]{0,1:T(8,128)} %param.11) | copy-start | bytes 2752516
  46.4 20.5 %copy-start.2 = (s32[2048,112]{0,1:T(8,128)S(1)}, s32[2048,112]{0,1:T(8,128)}, u32[]{:S(2)}) copy-start(s32[2048,112]{0,1:T(8,128)} %param.13) | copy-start | bytes 2752516
  101.6 23.7 %copy-start = (bf16[4,256,2048]{2,1,0:T(8,128)(2,1)S(1)}, bf16[4,256,2048]{2,1,0:T(8,128)(2,1)}, u32[]{:S(2)}) copy-start(bf16[4,256,2048]{2,1,0:T(8,128)(2,1)} %copy.18) | copy-start | bytes 12582916
  158.5 175.2 %all-gather.2.cloned.1.call-start = ((), (), s32[]{:S(2)}) async-start(), calls=%async_computation.4 | async-start | bytes 9175040 | tf_op jit(solution)/shard_map/all_gather | solution.py:40
  281.2 162.1 %reduce-scatter.5.cloned.1.call-start = ((), (), s32[]{:S(2)}) async-start(), calls=%async_computation.5 | async-start | bytes 4718592 | tf_op jit(solution)/shard_map/reduce_scatter | solution.py:44
  281.3 19.5 %copy-start.3 = (s32[3584,64]{0,1:T(8,128)S(1)}, s32[3584,64]{0,1:T(8,128)}, u32[]{:S(2)}) copy-start(s32[3584,64]{0,1:T(8,128)} %param.15) | copy-start | bytes 2752516
Sparse Core Ops, SparseCore 0:
  158.6 117.0 reduce-scatter.2
  281.3 52.2 all-gather.1
  355.0 88.2 reduce-scatter.4
where the time goes:
time: 452 us; the launch traced here: 450 us
  waiting for transfers between devices  208 us (46%)
  local copies, waits for them, and re-layouts  74.5 us (16%)
  other arithmetic  72 us (16%)
  matrix products  65.4 us (14%)
  between operations  13.8 us (3%)
  blocking collectives  10.6 us (2%)
  starting transfers between devices  5.01 us (1%)
    reduce_scatter x1, waiting for transfers between devices, on_device(): lax.psum_scatter(jnp.concatenate([gate_part, up_part], axis=1).astype(jnp...  117 us
    reduce_scatter x1, waiting for transfers between devices, on_device(): lax.psum_scatter(partial_out.astype(jnp.bfloat16), 'mp', scatter_dimensio...  73.5 us
    unnamed x14, local copies, waits for them, and re-layouts  66.7 us
    select_n x2, other arithmetic, keep_entries(): return jnp.where(kept_bits == 1, weight, jnp.zeros_like(weight))  43.5 us
    dot_general x1, matrix products, on_device(): gate_part = jnp.dot(columns, gate_kept, preferred_element_type=jnp.float32)  23.7 us
    dot_general x1, matrix products, on_device(): jnp.dot(lax.all_gather(hidden, 'dp', axis=0, tiled=True), down_kept, pref...  21.2 us
    dot_general x1, matrix products, on_device(): up_part = jnp.dot(columns, up_kept, preferred_element_type=jnp.float32)  20.5 us
    all_gather x1, waiting for transfers between devices, on_device(): lax.all_gather(hidden, 'dp', axis=0, tiled=True)  17.7 us
  transfers between devices with their start and end apart: 4, of which 3 were waited for; matrix products, arithmetic and copies ran while one was open for 24% of the time, Pallas kernels for 0%

commit v1 on v0

--- a/solution.py
+++ b/solution.py
@@ -2,6 +2,7 @@
 import jax.numpy as jnp
 from jax import lax
 from jax.sharding import PartitionSpec as P
+from jax.lax import all_to_all, axis_size
 
 
 def keep_entries(weight, packed):
@@ -36,11 +37,17 @@
     wide_hidden = hidden.astype(jnp.float32)
     squares = lax.psum(jnp.sum(wide_hidden * wide_hidden, axis=0), "dp")
     hidden_norms = jnp.sqrt(squares)
-    partial_out = jnp.dot(
-        lax.all_gather(hidden, "dp", axis=0, tiled=True),
-        down_kept,
-        preferred_element_type=jnp.float32,
-    )
+
+    def measure_ranges(local_values):
+        res = all_to_all(
+            jnp.stack(tuple((local_values for _ in range(axis_size("dp")))), 0),
+            concat_axis=0,
+            split_axis=0,
+            axis_name="dp",
+        )
+        return jnp.concatenate(res, 0)
+
+    partial_out = jnp.dot(measure_ranges(hidden), down_kept, preferred_element_type=jnp.float32)
     mixed = lax.psum_scatter(
         partial_out.astype(jnp.bfloat16), "mp", scatter_dimension=0, tiled=True
     )

time: 452 us -> 490 us (1.084)
  waiting for transfers between devices: 208 us -> 239 us
  starting transfers between devices: 5.01 us -> 10.4 us
    all_to_all x0 -> x1, waiting for transfers between devices: none -> 47.7 us  [measure_ranges(): all_to_all(jnp.stack(tuple((local_values for _ in range(axis_size('dp')))...]
    all_gather x1 -> x0, waiting for transfers between devices: 17.7 us -> none  [on_device(): lax.all_gather(hidden, 'dp', axis=0, tiled=True)]
    all_to_all x0 -> x1, starting transfers between devices: none -> 5.43 us  [measure_ranges(): all_to_all(jnp.stack(tuple((local_values for _ in range(axis_size('dp')))...]
  transfers between devices with their start and end apart: 4 -> 4, of which waited for: 3 -> 3; matrix products, arithmetic and copies ran while one was open for 24% -> 22% of each run, Pallas kernels for 0% -> 0%
where the time goes in v1:
time: 490 us; the launch traced here: 487 us
  waiting for transfers between devices  239 us (49%)
  local copies, waits for them, and re-layouts  77.4 us (16%)
  other arithmetic  70.8 us (14%)
  matrix products  65.5 us (13%)
  between operations  14.1 us (3%)
  blocking collectives  10.5 us (2%)
  starting transfers between devices  10.4 us (2%)
    reduce_scatter x1, waiting for transfers between devices, on_device(): lax.psum_scatter(jnp.concatenate([gate_part, up_part], axis=1).astype(jnp...  117 us
    reduce_scatter x1, waiting for transfers between devices, on_device(): lax.psum_scatter(partial_out.astype(jnp.bfloat16), 'mp', scatter_dimensio...  73.6 us
    unnamed x14, local copies, waits for them, and re-layouts  66.2 us
    all_to_all x1, waiting for transfers between devices, measure_ranges(): all_to_all(jnp.stack(tuple((local_values for _ in range(axis_size('dp')))...  47.7 us
    select_n x2, other arithmetic, keep_entries(): return jnp.where(kept_bits == 1, weight, jnp.zeros_like(weight))  43.4 us
    dot_general x1, matrix products, on_device(): gate_part = jnp.dot(columns, gate_kept, preferred_element_type=jnp.float32)  23.7 us
    dot_general x1, matrix products, on_device(): jnp.dot(measure_ranges(hidden), down_kept, preferred_element_type=jnp.flo...  21.2 us
    dot_general x1, matrix products, on_device(): up_part = jnp.dot(columns, up_kept, preferred_element_type=jnp.float32)  20.6 us
  transfers between devices with their start and end apart: 4, of which 3 were waited for; matrix products, arithmetic and copies ran while one was open for 22% of the time, Pallas kernels for 0%

profile of v1, /device:TPU:0, one launch (start us, length us, event | category | flops | bytes accessed | tf_op | source)
XLA Modules:
  0.0 487.3 jit_solution(17206727851068658818)
XLA Ops:
  7.2 6.4 %copy.17 = bf16[256,8192]{0,1:T(8,128)(2,1)} copy(bf16[256,8192]{1,0:T(8,128)(2,1)} %param.8) | data formatting | bytes 8388608 | tf_op args[0]
  13.6 3.3 fusion.9
  16.9 4.2 fusion.11
  21.0 4.9 %all-to-all-start = ((bf16[256,4,2048]{0,2,1:T(8,128)(2,1)}), bf16[256,4,2048]{0,2,1:T(8,128)(2,1)}, u32[]{:S(2)}, u32[]{:S(2)}) async-start(bf16[256,4,2048]{0,2,1:T(8,128)(2,1)} %bitcast.35), calls=%async_computation | async-start | bytes 8388608 | tf_op jit(solution)/shard_map/all_to_all | solution.py:21
  26.1 20.2 %copy.19 = bf16[2048,3584]{0,1:T(8,128)(2,1)} copy(bf16[2048,3584]{1,0:T(8,128)(2,1)} %param.10) | data formatting | bytes 29360128 | tf_op args[2]
  46.3 20.5 %copy.20 = bf16[2048,3584]{0,1:T(8,128)(2,1)} copy(bf16[2048,3584]{1,0:T(8,128)(2,1)} %param.12) | data formatting | bytes 29360128 | tf_op args[4]
  66.8 28.4 %fusion.6 = (bf16[2048,3584]{0,1:T(8,128)(2,1)}, bf16[2048,3584]{0,1:T(8,128)(2,1)}) fusion(bf16[2048,3584]{0,1:T(8,128)(2,1)} %copy.19, s32[3584]{0:T(1024)S(1)} %shift_right_arithmetic.63, s32[2048,112]{0,1:T(8,128)S(1)} %copy-done.1, bf16[2048,3584]{0,1:T(8,128)(2,1)} %copy.20, s32[2048,112]{0,1:T(8,128)S(1)} %copy-done.2), kind=kLoop, calls=%fused_computation.9 | loop fusion | flops 58720256 | bytes 60569600 | tf_op jit(solution)/shard_map/jit(_where)/select_n | solution.py:12
  95.2 6.3 %copy.18 = bf16[4,256,2048]{2,1,0:T(8,128)(2,1)} copy(bf16[4,256,2048]{1,2,0:T(8,128)(2,1)} %bitcast.1) | data formatting | bytes 8388608 | tf_op jit(solution)/shard_map/all_to_all | solution.py:21
  101.5 23.7 %convolution_convert_fusion.1 = bf16[1024,3584]{1,0:T(8,128)(2,1)} fusion(bf16[1024,2048]{1,0:T(8,128)(2,1)} %bitcast.36, bf16[2048,3584]{0,1:T(8,128)(2,1)} %get-tuple-element.5), kind=kOutput, calls=%fused_computation.20 | convolution fusion | flops 15036055552 | bytes 26214400 | tf_op jit(solution)/shard_map/dot_general | solution.py:28
  125.2 20.6 %convolution_convert_fusion = bf16[1024,3584]{1,0:T(8,128)(2,1)} fusion(bf16[1024,2048]{1,0:T(8,128)(2,1)S(1)} %bitcast.37, bf16[2048,3584]{0,1:T(8,128)(2,1)} %get-tuple-element.6), kind=kOutput, calls=%fused_computation.19 | convolution fusion | flops 15036055552 | bytes 26214400 | tf_op jit(solution)/shard_map/dot_general | solution.py:29
  145.8 12.6 %pad_maximum_fusion = bf16[1024,7168]{1,0:T(8,128)(2,1)} fusion(bf16[1024,3584]{1,0:T(8,128)(2,1)} %convolution_convert_fusion, bf16[1024,3584]{1,0:T(8,128)(2,1)} %convolution_convert_fusion.1), kind=kLoop, calls=%fused_computation.12 | loop fusion | flops 29360128 | bytes 29360128 | tf_op jit(solution)/shard_map/concatenate | solution.py:31
  158.4 117.3 %reduce-scatter.3.cloned.1.call-done = bf16[256,7168]{1,0:T(8,128)(2,1)} async-done(((bf16[1024,7168]{1,0:T(8,128)(2,1)}), bf16[256,7168]{1,0:T(8,128)(2,1)}) %reduce-scatter.3.cloned.1.call-update) | async-done | bytes 3670032 | tf_op jit(solution)/shard_map/reduce_scatter | solution.py:30
  275.7 2.9 convert_element_type.25
  278.6 1.3 multiply_reduce_fusion.1
  279.9 3.5 stack.2
  283.4 5.4 %all-to-all-start.1 = ((bf16[4,256,3584]{2,1,0:T(8,128)(2,1)}), bf16[4,256,3584]{2,1,0:T(8,128)(2,1)}, u32[]{:S(2)}, u32[]{:S(2)}) async-start(bf16[4,256,3584]{2,1,0:T(8,128)(2,1)} %stack.2), calls=%async_computation.2 | async-start | bytes 14680064 | tf_op jit(solution)/shard_map/all_to_all | solution.py:42
  289.0 19.1 %copy.21 = bf16[3584,2048]{0,1:T(8,128)(2,1)} copy(bf16[3584,2048]{1,0:T(8,128)(2,1)} %param.14) | data formatting | bytes 29360128 | tf_op args[6]
  308.1 15.1 %fusion.8 = bf16[3584,2048]{0,1:T(8,128)(2,1)} fusion(bf16[3584,2048]{0,1:T(8,128)(2,1)} %copy.21, s32[2048]{0:T(1024)S(1)} %shift_right_arithmetic.72, s32[3584,64]{0,1:T(8,128)S(1)} %copy-done.3), kind=kLoop, calls=%fused_computation.11 | loop fusion | flops 29360128 | bytes 30285824 | tf_op jit(solution)/shard_map/jit(_where)/select_n | solution.py:12
  323.1 47.7 %all-to-all-done.1 = bf16[4,256,3584]{2,1,0:T(8,128)(2,1)} async-done(((bf16[4,256,3584]{2,1,0:T(8,128)(2,1)}), bf16[4,256,3584]{2,1,0:T(8,128)(2,1)}, u32[]{:S(2)}, u32[]{:S(2)}) %all-to-all-start.1) | async-done | bytes 7340064 | tf_op jit(solution)/shard_map/all_to_all | solution.py:42
  370.8 21.2 %convolution_convert_fusion.2 = bf16[1024,2048]{1,0:T(8,128)(2,1)} fusion(bf16[1024,3584]{1,0:T(8,128)(2,1)} %bitcast.5, bf16[3584,2048]{0,1:T(8,128)(2,1)} %fusion.8), kind=kOutput, calls=%fused_computation.21 | convolution fusion | flops 15034482688 | bytes 26214400 | tf_op jit(solution)/shard_map/dot_general | solution.py:50
  392.0 3.1 multiply_reduce_fusion
  395.7 10.5 %psum.7 = f32[3584]{0:T(1024)S(1)} all-reduce(f32[3584]{0:T(1024)S(1)} %get-tuple-element.3), channel_id=1, replica_groups=mesh['dp'=4,'mp'=8] {'dp'}, use_global_device_ids=true, to_apply=%region_5.6 | all-reduce | flops 3584 | bytes 28672 | tf_op jit(solution)/shard_map/psum | solution.py:38
  406.2 0.6 sqrt.7
  406.8 73.6 %reduce-scatter.5.cloned.1.call-done = bf16[128,2048]{1,0:T(8,128)(2,1)} async-done(((bf16[1024,2048]{1,0:T(8,128)(2,1)}), bf16[128,2048]{1,0:T(8,128)(2,1)}) %reduce-scatter.5.cloned.1.call-update) | async-done | bytes 524304 | tf_op jit(solution)/shard_map/reduce_scatter | solution.py:51
  (21 shorter events, 0.9 us)
Async XLA Ops:
  7.2 9.7 %copy-start.4 = (f32[8192]{0:T(1024)S(1)}, f32[8192]{0:T(1024)}, u32[]{:S(2)}) copy-start(f32[8192]{0:T(1024)} %param.9) | copy-start | bytes 98308
  21.0 74.2 %all-to-all-start = ((bf16[256,4,2048]{0,2,1:T(8,128)(2,1)}), bf16[256,4,2048]{0,2,1:T(8,128)(2,1)}, u32[]{:S(2)}, u32[]{:S(2)}) async-start(bf16[256,4,2048]{0,2,1:T(8,128)(2,1)} %bitcast.35), calls=%async_computation | async-start | bytes 8388608 | tf_op jit(solution)/shard_map/all_to_all | solution.py:21
  25.9 249.8 %reduce-scatter.3.cloned.1.call-start = ((), (), s32[]{:S(2)}) async-start(), calls=%async_computation.4 | async-start | bytes 18350080 | tf_op jit(solution)/shard_map/reduce_scatter | solution.py:30
  46.3 20.5 %copy-start.1 = (s32[2048,112]{0,1:T(8,128)S(1)}, s32[2048,112]{0,1:T(8,128)}, u32[]{:S(2)}) copy-start(s32[2048,112]{0,1:T(8,128)} %param.11) | copy-start | bytes 2752516
  46.3 20.5 %copy-start.2 = (s32[2048,112]{0,1:T(8,128)S(1)}, s32[2048,112]{0,1:T(8,128)}, u32[]{:S(2)}) copy-start(s32[2048,112]{0,1:T(8,128)} %param.13) | copy-start | bytes 2752516
  101.5 23.7 %copy-start = (bf16[4,256,2048]{2,1,0:T(8,128)(2,1)S(1)}, bf16[4,256,2048]{2,1,0:T(8,128)(2,1)}, u32[]{:S(2)}) copy-start(bf16[4,256,2048]{2,1,0:T(8,128)(2,1)} %copy.18) | copy-start | bytes 12582916
  283.4 87.3 %all-to-all-start.1 = ((bf16[4,256,3584]{2,1,0:T(8,128)(2,1)}), bf16[4,256,3584]{2,1,0:T(8,128)(2,1)}, u32[]{:S(2)}, u32[]{:S(2)}) async-start(bf16[4,256,3584]{2,1,0:T(8,128)(2,1)} %stack.2), calls=%async_computation.2 | async-start | bytes 14680064 | tf_op jit(solution)/shard_map/all_to_all | solution.py:42
  288.9 191.6 %reduce-scatter.5.cloned.1.call-start = ((), (), s32[]{:S(2)}) async-start(), calls=%async_computation.5 | async-start | bytes 4718592 | tf_op jit(solution)/shard_map/reduce_scatter | solution.py:51
  289.0 19.1 %copy-start.3 = (s32[3584,64]{0,1:T(8,128)S(1)}, s32[3584,64]{0,1:T(8,128)}, u32[]{:S(2)}) copy-start(s32[3584,64]{0,1:T(8,128)} %param.15) | copy-start | bytes 2752516
Sparse Core Ops, SparseCore 0:
  158.6 117.0 reduce-scatter.2
  392.1 88.2 reduce-scatter.4
